TPU v7x, 8 devices: a whole 2x2x1 slice. The times are simulated.
8 devices in a mesh: data: 2 (over z, y), stage: 4 (over x, core).
Axes of the slice: x: 2, y: 2, z: 1, core: 2. Of those that a mesh axis runs over, the one named last changes fastest.
Arguments:
- x: bfloat16 [32, 512, 1024], P('data'), parts along dimension 0
- g: bfloat16 [32, 512, 1024], P('data'), parts along dimension 0
- w1: bfloat16 [2, 4, 1024, 4096], P(None, 'stage')
- w2: bfloat16 [2, 4, 4096, 1024], P(None, 'stage')
Outputs:
- output 1: bfloat16 [32, 512, 1024], P('data'), parts along dimension 0
- output 2: bfloat16 [32, 512, 1024], P('data'), parts along dimension 0
- output 3: float32 [4, 4, 1024, 4096], P('data', 'stage'), parts along dimension 0
- output 4: float32 [4, 4, 4096, 1024], P('data', 'stage'), parts along dimension 0
There are 2 independent parts. A program takes and returns all parts, laid end to end along the dimension named above; an argument that names none is the same for every part.
All inputs are finite; a program needn't handle non-finite values.
Results may differ from a plain program's by a relative error of at most 0.02.
Values are sent between devices in bfloat16 or wider.
A program may use at most 1 GiB of HBM per device.

v0:
```python
import jax
import jax.numpy as jnp
from jax import lax
from jax.sharding import PartitionSpec as P


def _gelu(z):
    return 0.5 * z * (1.0 + lax.erf(z * 0.7071067811865476))


def _gelu_grad(z):
    return 0.5 * (1.0 + lax.erf(z * 0.7071067811865476)) + z * jnp.exp(-0.5 * z * z) * 0.3989422804014327


def _gelu_pair(z):
    e = lax.erf(z * 0.7071067811865476)
    return 0.5 * z * (1.0 + e), 0.5 * (1.0 + e) + z * jnp.exp(-0.5 * z * z) * 0.3989422804014327


def _fwd(h, w1, w2):
    z = jnp.dot(h, w1, preferred_element_type=jnp.float32)
    u = _gelu(z).astype(jnp.bfloat16)
    r = jnp.dot(u, w2, preferred_element_type=jnp.float32)
    return (h.astype(jnp.float32) + r).astype(jnp.bfloat16)


def _bwd(h, w1, w2, dy):
    nt = (((1,), (1,)), ((), ()))
    z = jnp.dot(h, w1, preferred_element_type=jnp.float32)
    a, b = _gelu_pair(z)
    u = a.astype(jnp.bfloat16)
    du = lax.dot_general(dy, w2, nt, preferred_element_type=jnp.float32)
    dz = (du * b).astype(jnp.bfloat16)
    dh = (dy.astype(jnp.float32) + lax.dot_general(dz, w1, nt, preferred_element_type=jnp.float32)).astype(jnp.bfloat16)
    return dh, u, dz


def _hits(ts, S, M, V):
    out = []
    for vv in range(V):
        seen = [0 <= t - S + 1 + q < V * M and V - 1 - (t - S + 1 + q) // M == vv for t in ts for q in range(S)]
        if any(seen):
            out.append((vv, all(seen)))
    return out


def _acc(d1, d2, rows, hits):
    tn = (((0,), (0,)), ((), ()))
    h, u, dz, dy = [jnp.stack([r[k] for r in rows]) for k in range(2, 6)]
    for vv, full in hits:
        hm, ym = h, dy
        if not full:
            sel = jnp.stack([r[1] & (r[0] == vv) for r in rows])[:, None, None]
            hm = jnp.where(sel, h, 0)
            ym = jnp.where(sel, dy, 0)
        d1 = d1.at[vv].add(lax.dot_general(hm.reshape(-1, hm.shape[-1]), dz.reshape(-1, dz.shape[-1]), tn, preferred_element_type=jnp.float32))
        d2 = d2.at[vv].add(lax.dot_general(u.reshape(-1, u.shape[-1]), ym.reshape(-1, ym.shape[-1]), tn, preferred_element_type=jnp.float32))
    return d1, d2


def solution(mesh):
    S = mesh.shape['stage']
    fwd_pairs = [(j, (j + 1) % S) for j in range(S)]
    bwd_pairs = [(j, (j - 1) % S) for j in range(S)]

    def body(x, g, w1, w2):
        M, B, D = x.shape
        V = w1.shape[0]
        w1 = w1[:, 0]
        w2 = w2[:, 0]
        VM = V * M
        T = VM + S - 1
        p = lax.axis_index('stage')
        first = p == 0
        last = p == S - 1
        saved = jnp.zeros((V, M, B, D), x.dtype)
        wrap = jnp.zeros((M, B, D), x.dtype)
        ybuf = jnp.zeros((M, B, D), x.dtype)
        recv = jnp.zeros((B, D), x.dtype)
        for t in range(T):
            i = t - p
            valid = (i >= 0) & (i < VM)
            ic = jnp.clip(i, 0, VM - 1)
            v, m = ic // M, ic % M
            hin = jnp.where(first, jnp.where(v == 0, x[m], wrap[m]), recv)
            saved = saved.at[v, m].set(jnp.where(valid, hin, saved[v, m]))
            hout = _fwd(hin, w1[v], w2[v])
            ybuf = ybuf.at[m].set(jnp.where(valid & last & (v == V - 1), hout, ybuf[m]))
            recv = lax.ppermute(hout, 'stage', fwd_pairs)
            j = t - (S - 1)
            if 0 <= j < VM - M:
                wrap = wrap.at[j % M].set(recv)
        dxbuf = jnp.zeros((M, B, D), x.dtype)
        d1 = jnp.zeros(w1.shape, jnp.float32)
        d2 = jnp.zeros(w2.shape, jnp.float32)
        wrapb = jnp.zeros((M, B, D), x.dtype)
        recv = jnp.zeros((B, D), x.dtype)
        rows, ts = [], []
        for t in range(T):
            i = t - (S - 1 - p)
            valid = (i >= 0) & (i < VM)
            ic = jnp.clip(i, 0, VM - 1)
            v, m = V - 1 - ic // M, ic % M
            dy = jnp.where(last, jnp.where(v == V - 1, g[m], wrapb[m]), recv)
            h = saved[v, m]
            dh, u, dz = _bwd(h, w1[v], w2[v], dy)
            rows.append((v, valid, h, u, dz, dy))
            ts.append(t)
            if len(ts) == S or t == T - 1:
                d1, d2 = _acc(d1, d2, rows, _hits(ts, S, M, V))
                rows, ts = [], []
            dxbuf = dxbuf.at[m].set(jnp.where(valid & first & (v == 0), dh, dxbuf[m]))
            recv = lax.ppermute(dh, 'stage', bwd_pairs)
            j = t - (S - 1)
            if 0 <= j < VM - M:
                wrapb = wrapb.at[j % M].set(recv)
        y = lax.psum(ybuf, 'stage')
        dx = lax.psum(dxbuf, 'stage')
        return y, dx, d1[:, None], d2[:, None]

    act = P('data', None, None)
    wsp = P(None, 'stage', None, None)
    gsp = P('data', 'stage', None, None)
    return jax.shard_map(body, mesh=mesh, in_specs=(act, act, wsp, wsp), out_specs=(act, act, gsp, gsp), check_vma=False)
```

profile of v0, /device:TPU:0, one launch (start us, length us, event | category | flops | bytes accessed | tf_op | source)
XLA Modules:
  0.0 3972.8 jit_solution(16349133151649009006)
XLA Ops:
  46.9 18.0 fusion.1561
  79.1 17.5 fusion.1560
  116.7 17.7 fusion.1559
  148.9 18.0 fusion.1558
  336.3 17.2 fusion.1553
  481.8 17.2 fusion.1549
  735.5 17.0 fusion.1542
  805.8 17.2 fusion.1540
  946.6 17.2 fusion.1536
  2375.3 26.1 fusion.60
  2427.9 25.4 fusion.4
  2453.3 23.9 scatter-add.84
  2516.8 31.2 bitcast_dynamic-update-slice_fusion.10
  2573.5 31.3 bitcast_dynamic-update-slice_fusion.13
  2630.7 31.2 bitcast_dynamic-update-slice_fusion.9
  2687.4 31.3 bitcast_dynamic-update-slice_fusion.12
  2745.8 25.5 bitcast_dynamic-update-slice_fusion.8
  2796.8 27.4 bitcast_dynamic-update-slice_fusion.11
  2850.5 26.4 fusion.1
  2901.6 26.2 fusion
  2954.9 28.0 fusion.3
  3007.5 28.2 fusion.2
  3035.7 24.8 copy.245
  3105.3 31.3 bitcast_dynamic-update-slice_fusion.3
  3162.0 31.2 bitcast_dynamic-update-slice_fusion.7
  3220.0 31.3 bitcast_dynamic-update-slice_fusion.2
  3276.8 31.3 bitcast_dynamic-update-slice_fusion.6
  3334.0 31.3 bitcast_dynamic-update-slice_fusion.5
  3391.1 31.2 bitcast_dynamic-update-slice_fusion.1
  3422.3 24.3 bitcast_dynamic-update-slice_fusion
  3446.6 22.7 bitcast_dynamic-update-slice_fusion.4
  3469.3 473.1 %all-reduce.7.cloned.1.call-done = (bf16[16,512,1024]{2,1,0:T(8,128)(2,1)}, bf16[16,512,1024]{2,1,0:T(8,128)(2,1)}) async-done(((bf16[16,512,1024]{2,1,0:T(8,128)(2,1)}, bf16[16,512,1024]{2,1,0:T(8,128)(2,1)}), (bf16[16,512,1024]{2,1,0:T(8,128)(2,1)}, bf16[16,512,1024]{2,1,0:T(8,128)(2,1)})) %all-reduce.7.cloned.1.call-update) | async-done | bytes 33554448 | tf_op jit(solution)/shard_map/psum | solution.py:117
  (970 shorter events, 2703.4 us)
Async XLA Ops:
  7.2 3935.3 %all-reduce.7.cloned.1.call-start = ((), (), s32[]{:S(2)}) async-start(), calls=%async_computation | async-start | bytes 67108864 | tf_op jit(solution)/shard_map/psum | solution.py:117
  31.7 15.3 collective-permute-start
  96.6 20.1 collective-permute-start.2
  134.3 14.6 collective-permute-start.3
  1491.3 111.5 %collective-permute-start.34 = (bf16[512,1024]{1,0:T(8,128)(2,1)}, bf16[512,1024]{1,0:T(8,128)(2,1)}, u32[]{:S(2)}, u32[]{:S(2)}) collective-permute-start(bf16[512,1024]{1,0:T(8,128)(2,1)} %get-tuple-element.2200), channel_id=1, source_target_pairs={{0,3},{1,0},{2,1},{3,2},{4,7},{5,4},{6,5},{7,6}} | collective-permute-start | bytes 3145736 | tf_op jit(solution)/shard_map/ppermute | solution.py:113
  1629.5 15.1 collective-permute-start.35
  1667.1 21.5 collective-permute-start.36
  1751.7 25.0 collective-permute-start.38
  1839.2 26.1 collective-permute-start.40
  1928.0 25.9 collective-permute-start.42
  1978.4 24.4 collective-permute-start.43
  2032.4 28.1 collective-permute-start.44
  2124.2 37.9 collective-permute-start.46
  2186.3 26.3 collective-permute-start.47
  2276.5 34.1 collective-permute-start.49
  2373.4 29.3 collective-permute-start.51
  2427.8 62.4 %collective-permute-start.52 = (bf16[512,1024]{1,0:T(8,128)(2,1)S(1)}, bf16[512,1024]{1,0:T(8,128)(2,1)S(1)}, u32[]{:S(2)}, u32[]{:S(2)}) collective-permute-start(bf16[512,1024]{1,0:T(8,128)(2,1)S(1)} %get-tuple-element.2236), channel_id=1, source_target_pairs={{0,3},{1,0},{2,1},{3,2},{4,7},{5,4},{6,5},{7,6}} | collective-permute-start | bytes 3145736 | tf_op jit(solution)/shard_map/ppermute | solution.py:113
  2515.1 34.1 collective-permute-start.53
  2573.4 32.6 collective-permute-start.54
  2630.2 33.1 collective-permute-start.55
  2687.3 32.6 collective-permute-start.56
  2744.2 28.4 collective-permute-start.57
  2796.8 28.7 collective-permute-start.58
  2849.9 28.3 collective-permute-start.59
  2901.6 27.5 collective-permute-start.60
  2953.6 30.6 collective-permute-start.61
  3007.2 73.3 %collective-permute-start.62 = (bf16[512,1024]{1,0:T(8,128)(2,1)S(1)}, bf16[512,1024]{1,0:T(8,128)(2,1)S(1)}, u32[]{:S(2)}, u32[]{:S(2)}) collective-permute-start(bf16[512,1024]{1,0:T(8,128)(2,1)S(1)} %get-tuple-element.2256), channel_id=1, source_target_pairs={{0,3},{1,0},{2,1},{3,2},{4,7},{5,4},{6,5},{7,6}} | collective-permute-start | bytes 3145736 | tf_op jit(solution)/shard_map/ppermute | solution.py:113
  3104.8 33.1 collective-permute-start.63
  3162.0 32.6 collective-permute-start.64
  3218.7 33.9 collective-permute-start.65
  3276.7 32.6 collective-permute-start.66
  3333.1 33.6 collective-permute-start.67
  (227 other events, 3683.7 us)
Sparse Core Ops, SparseCore 0:
  3389.4 553.0 all-reduce.6
where the time goes:
time: 3990 us; the launch traced here: 3970 us
  matrix products  2320 us (58%)
  waiting for transfers between devices  818 us (21%)
  other arithmetic  387 us (10%)
  local copies, waits for them, and re-layouts  386 us (10%)
  starting transfers between devices  47.4 us (1%)
    dot_general x35, matrix products, _fwd(): r = jnp.dot(u, w2, preferred_element_type=jnp.float32)  593 us
    psum x1, waiting for transfers between devices, body(): y = lax.psum(ybuf, 'stage')  473 us
    dot_general x35, matrix products, _bwd(): du = lax.dot_general(dy, w2, nt, preferred_element_type=jnp.float32)  395 us
    dot_general x35, matrix products, _bwd(): lax.dot_general(dz, w1, nt, preferred_element_type=jnp.float32)  390 us
    dot_general x35, matrix products, _bwd(): z = jnp.dot(h, w1, preferred_element_type=jnp.float32)  366 us
    ppermute x34, waiting for transfers between devices, body(): recv = lax.ppermute(hout, 'stage', fwd_pairs)  318 us
    dot_general x10, matrix products, _acc(): lax.dot_general(hm.reshape(-1, hm.shape[-1]), dz.reshape(-1, dz.shape[-1]...  288 us
    dot_general x10, matrix products, _acc(): lax.dot_general(u.reshape(-1, u.shape[-1]), ym.reshape(-1, ym.shape[-1]),...  285 us
  transfers between devices with their start and end apart: 69, of which 39 were waited for; matrix products, arithmetic and copies ran while one was open for 31% of the time, Pallas kernels for 0%

commit v1 on v0

v1 whole, which is shorter than its diff:
```python
import functools

import jax
import jax.numpy as jnp
from jax import lax
from jax.experimental import pallas as pl
from jax.experimental.pallas import tpu as pltpu
from jax.sharding import PartitionSpec as P

MESH = pl.DeviceIdType.MESH
ANY = pl.ANY
BF = jnp.bfloat16
F32 = jnp.float32
VMEM_LIMIT = 67043328
NT = (((1,), (1,)), ((), ()))
TN = (((0,), (0,)), ((), ()))
HOUT = 4
DHO = 2


def _gelu(z):
    return 0.5 * z * (1.0 + lax.erf(z * 0.7071067811865476))


def _gelu_pair(z):
    half = 0.5 * (1.0 + lax.erf(z * 0.7071067811865476))
    return z * half, half + z * jnp.exp(-0.5 * z * z) * 0.3989422804014327


def _pipe_kernel(S, V, M, B, D, F, G, W0, WSTEP, YD, DXD, NS, FB,
                 x, g, w1, w2,
                 hs, dys, us, dzs, yo, dxo,
                 w1v, w2v, hin, hout, uf, hb, dyb, zb, ubuf, dzbuf, dho,
                 wsem, finsem, frecv, fsend, ysem, yrecv, yfwd,
                 hbsem, dysem, uosem, brecv, bsend, dxsem, dxrecv, dxfwd):
    p = lax.axis_index('stage')
    right = lax.rem(p + 1, S)
    left = lax.rem(p + S - 1, S)
    N = V * M
    HB = B // 2
    wp = W0 + WSTEP * (S - 1 - p)
    is_last = lax.div(p + 1, S)
    is_first = 1 - lax.div(p + S - 1, S)

    def unit_f(i):
        gi = lax.div(i, V * G)
        rem = lax.rem(i, V * G)
        return lax.div(rem, G), gi * G + lax.rem(rem, G)

    def unit_b(i):
        v, m = unit_f(i)
        return V - 1 - v, m

    def rdma(src, dst, ssem, rsem, to):
        return pltpu.make_async_remote_copy(src_ref=src, dst_ref=dst, send_sem=ssem, recv_sem=rsem,
                                            device_id={'stage': to}, device_id_type=MESH)

    def rows(q):
        return pl.ds(pl.multiple_of(q * HB, HB), HB)

    def f_send(s, v, m, q):
        sl = lax.rem(s, HOUT)
        return rdma(hout.at[sl, rows(q)], hs.at[v + is_last, m, rows(q)],
                    fsend.at[sl, q], frecv.at[v + is_last, m, q], right)

    def f_recv(v, m, q):
        return rdma(hout.at[0, rows(q)], hs.at[v, m, rows(q)], fsend.at[0, q], frecv.at[v, m, q], right)

    def f_load_x(s, m, q):
        sl = lax.rem(s, 2)
        return pltpu.make_async_copy(x.at[m, rows(q)], hin.at[sl, rows(q)], finsem.at[sl, q])

    def f_load_h(s, v, m, q):
        sl = lax.rem(s, 2)
        return pltpu.make_async_copy(hs.at[v, m, rows(q)], hin.at[sl, rows(q)], finsem.at[sl, q])

    def y_copies(s, m):
        sl = lax.rem(s, HOUT)
        return (pltpu.make_async_copy(hout.at[sl], yo.at[m], ysem.at[sl, 0]),
                rdma(hout.at[sl], yo.at[m], ysem.at[sl, 1], yrecv.at[m], left),
                rdma(hout.at[sl], yo.at[m], ysem.at[sl, 2], yrecv.at[m], right))

    def f_out_wait(s):
        v, m = unit_f(s)
        final = (is_last == 1) & (v == V - 1)

        @pl.when(final)
        def _():
            a, b, c = y_copies(s, m)
            a.wait()
            b.wait_send()
            c.wait_send()

        @pl.when(jnp.logical_not(final))
        def _():
            f_send(s, v, m, 0).wait_send()
            f_send(s, v, m, 1).wait_send()

    def b_send(b, v, m):
        sl = lax.rem(b, DHO)
        return rdma(dho.at[sl], dys.at[v - is_first, m], bsend.at[sl], brecv.at[v - is_first, m], left)

    def b_recv(v, m):
        return rdma(dho.at[0], dys.at[v, m], bsend.at[0], brecv.at[v, m], left)

    def dx_copies(b, m):
        sl = lax.rem(b, DHO)
        return (pltpu.make_async_copy(dho.at[sl], dxo.at[m], dxsem.at[sl, 0]),
                rdma(dho.at[sl], dxo.at[m], dxsem.at[sl, 1], dxrecv.at[m], left),
                rdma(dho.at[sl], dxo.at[m], dxsem.at[sl, 2], dxrecv.at[m], right))

    def b_out_wait(b):
        v, m = unit_b(b)
        final = (is_first == 1) & (v == 0)

        @pl.when(final)
        def _():
            a, c, d = dx_copies(b, m)
            a.wait()
            c.wait_send()
            d.wait_send()

        @pl.when(jnp.logical_not(final))
        def _():
            b_send(b, v, m).wait_send()

    def hb_start(b):
        v, m = unit_b(b)
        sl = lax.rem(b, 2)
        own = (is_first == 1) & (v == 0)

        @pl.when(own)
        def _():
            pltpu.make_async_copy(x.at[m], hb.at[sl], hbsem.at[sl]).start()

        @pl.when(jnp.logical_not(own))
        def _():
            pltpu.make_async_copy(hs.at[v, m], hb.at[sl], hbsem.at[sl]).start()

    def u_out(v, m):
        return (pltpu.make_async_copy(ubuf, us.at[v, m], uosem.at[0]),
                pltpu.make_async_copy(dzbuf, dzs.at[v, m], uosem.at[1]))

    def w_copies(v):
        return (pltpu.make_async_copy(w1.at[v], w1v.at[v], wsem.at[v, 0]),
                pltpu.make_async_copy(w2.at[v], w2v.at[v], wsem.at[v, 1]))

    @pl.when(is_first == 1)
    def _():
        f_load_x(0, 0, 0).start()
        f_load_x(0, 0, 1).start()

    for v in range(V):
        for c in w_copies(v):
            c.start()

    barrier = pltpu.get_barrier_semaphore()
    for nb in (left, right):
        pl.semaphore_signal(barrier, inc=1, device_id={'stage': nb}, device_id_type=MESH)
    pl.semaphore_wait(barrier, 2)

    for c in w_copies(0):
        c.wait()

    def slot(s, carry):
        @pl.when(s == G)
        def _():
            for v in range(1, V):
                for c in w_copies(v):
                    c.wait()

        def y_forward(i):
            v, m = unit_f(i)
            return (i >= 0) & (i < N) & (v == V - 1) & (is_first == 1), m

        def dx_forward(i):
            v, m = unit_b(i)
            return (i >= 0) & (i < N) & (v == 0) & (is_last == 1), m

        def y_fwd(m):
            return rdma(yo.at[m], yo.at[m], yfwd, yrecv.at[m], right)

        def dx_fwd(m):
            return rdma(dxo.at[m], dxo.at[m], dxfwd, dxrecv.at[m], left)

        was, mo = y_forward(s - 1 - YD)

        @pl.when(was)
        def _():
            y_fwd(mo).wait_send()

        was, mo = dx_forward(s - 1 - DXD)

        @pl.when(was)
        def _():
            dx_fwd(mo).wait_send()

        now, mn = y_forward(s - YD)

        @pl.when(now)
        def _():
            y_fwd(mn).wait_recv()
            y_fwd(mn).start()

        now, mn = dx_forward(s - DXD)

        @pl.when(now)
        def _():
            dx_fwd(mn).wait_recv()
            dx_fwd(mn).start()

        b = s - wp
        has_b = (b >= 0) & (b < N)
        has_f = s < N
        fv, fm = unit_f(s)
        f_own = (is_first == 1) & (fv == 0)

        @pl.when(has_f & has_b & f_own)
        def _():
            f_load_x(s, fm, 0).start()
            f_load_x(s, fm, 1).start()

        @pl.when(has_f & has_b & jnp.logical_not(f_own))
        def _():
            for q in range(2):
                f_recv(fv, fm, q).wait_recv()
                f_load_h(s, fv, fm, q).start()

        @pl.when(has_b)
        def _():
            v, m = unit_b(b)
            sl = lax.rem(b, 2)
            so = lax.rem(b, DHO)
            top = (is_last == 1) & (v == V - 1)

            @pl.when(top)
            def _():
                pltpu.make_async_copy(g.at[m], dyb, dysem).start()

            @pl.when(jnp.logical_not(top))
            def _():
                b_recv(v, m).wait_recv()
                pltpu.make_async_copy(dys.at[v, m], dyb, dysem).start()

            @pl.when(b == 0)
            def _():
                hb_start(b)

            @pl.when((s >= N) & (b + 1 < N))
            def _():
                hb_start(b + 1)

            @pl.when(b >= 1)
            def _():
                vo, mo = unit_b(b - 1)
                for c in u_out(vo, mo):
                    c.wait()

            @pl.when(b >= DHO)
            def _():
                b_out_wait(b - DHO)

            pltpu.make_async_copy(hs.at[v, m], hb.at[sl], hbsem.at[sl]).wait()
            h = hb[sl]
            zb[...] = jnp.dot(h, w1v[v, :, 0:FB], preferred_element_type=F32)
            pltpu.make_async_copy(g.at[m], dyb, dysem).wait()
            dy = dyb[...]
            for c in range(F // FB):
                cols = slice(c * FB, (c + 1) * FB)
                if c == 0:
                    z = zb[...]
                else:
                    z = jnp.dot(h, w1v[v, :, cols], preferred_element_type=F32)
                u, d = _gelu_pair(z)
                ubuf[:, cols] = u.astype(BF)
                du = lax.dot_general(dy, w2v[v, cols, :], NT, preferred_element_type=F32)
                dzbuf[:, cols] = (du * d).astype(BF)
            for c in u_out(v, m):
                c.start()
            r = lax.dot_general(dzbuf[...], w1v[v], NT, preferred_element_type=F32)
            dho[so] = (dy.astype(F32) + r).astype(BF)

            final = (is_first == 1) & (v == 0)

            @pl.when(final)
            def _():
                for c in dx_copies(b, m):
                    c.start()

            @pl.when(jnp.logical_not(final))
            def _():
                b_send(b, v, m).start()

        @pl.when(has_f)
        def _():
            sl = lax.rem(s, 2)
            so = lax.rem(s, HOUT)
            y_unit = (is_last == 1) & (fv == V - 1)

            @pl.when(s >= HOUT)
            def _():
                f_out_wait(s - HOUT)

            nv, nm = unit_f(s + 1)

            @pl.when((s + 1 < wp) & (is_first == 1) & (nv == 0))
            def _():
                f_load_x(s + 1, nm, 0).start()
                f_load_x(s + 1, nm, 1).start()

            def half(q, c2):
                @pl.when(jnp.logical_not(has_b) & jnp.logical_not(f_own))
                def _():
                    f_recv(fv, fm, q).wait_recv()
                    f_load_h(s, fv, fm, q).start()

                f_load_x(s, fm, q).wait()

                @pl.when((q == 1) & (s + 1 - wp >= 1) & (s + 1 - wp < N))
                def _():
                    hb_start(s + 1 - wp)

                h = hin[sl, rows(q), :]
                for c in range(F // FB):
                    cols = slice(c * FB, (c + 1) * FB)
                    z = jnp.dot(h, w1v[fv, :, cols], preferred_element_type=F32)
                    uf[:, cols] = _gelu(z).astype(BF)
                r = jnp.dot(uf[...], w2v[fv], preferred_element_type=F32)
                hout[so, rows(q), :] = (h.astype(F32) + r).astype(BF)

                @pl.when(jnp.logical_not(y_unit))
                def _():
                    f_send(s, fv, fm, q).start()

                return c2

            lax.fori_loop(0, 2, half, 0)

            @pl.when(y_unit)
            def _():
                for c in y_copies(s, fm):
                    c.start()

        return carry

    lax.fori_loop(0, NS, slot, 0)

    for i in range(N - HOUT, N):
        f_out_wait(i)
    for i in range(N - DHO, N):
        b_out_wait(i)
    vo, mo = unit_b(N - 1)
    for c in u_out(vo, mo):
        c.wait()

    mid = (is_first == 0) & (is_last == 0)

    def drain(m, carry):
        @pl.when(mid)
        def _():
            rdma(yo.at[m], yo.at[m], yfwd, yrecv.at[m], right).wait_recv()
            rdma(dxo.at[m], dxo.at[m], dxfwd, dxrecv.at[m], left).wait_recv()

        return carry

    lax.fori_loop(0, M, drain, 0)


def _pipe(x, g, w1, w2, S):
    M, B, D = x.shape
    V, _, F = w1.shape
    N = V * M
    G = M // 2
    W0, WSTEP = G + 1, 3
    YD, DXD = 8, 16
    NS = max(N + W0 + WSTEP * (S - 1), N + DXD + 1, N + YD + 1)
    FB = F // 4
    kern = functools.partial(_pipe_kernel, S, V, M, B, D, F, G, W0, WSTEP, YD, DXD, NS, FB)
    act = jax.ShapeDtypeStruct((V, M, B, D), BF)
    wide = jax.ShapeDtypeStruct((V, M, B, F), BF)
    out = jax.ShapeDtypeStruct((M, B, D), BF)
    DMA = pltpu.SemaphoreType.DMA
    flops = N * 10 * B * D * F
    return pl.pallas_call(
        kern,
        out_shape=(act, act, wide, wide, out, out),
        in_specs=[pl.BlockSpec(memory_space=ANY)] * 4,
        out_specs=[pl.BlockSpec(memory_space=ANY)] * 6,
        scratch_shapes=[
            pltpu.VMEM((V, D, F), BF), pltpu.VMEM((V, F, D), BF),
            pltpu.VMEM((2, B, D), BF), pltpu.VMEM((HOUT, B, D), BF), pltpu.VMEM((B // 2, F), BF),
            pltpu.VMEM((2, B, D), BF), pltpu.VMEM((B, D), BF), pltpu.VMEM((B, FB), F32),
            pltpu.VMEM((B, F), BF), pltpu.VMEM((B, F), BF), pltpu.VMEM((DHO, B, D), BF),
            DMA((V, 2)), DMA((2, 2)), DMA((V, M, 2)), DMA((HOUT, 2)), DMA((HOUT, 3)), DMA((M,)), DMA,
            DMA((2,)), DMA, DMA((2,)), DMA((V, M)), DMA((DHO,)), DMA((DHO, 3)), DMA((M,)), DMA,
        ],
        compiler_params=pltpu.CompilerParams(collective_id=0, has_side_effects=True, vmem_limit_bytes=VMEM_LIMIT),
        cost_estimate=pl.CostEstimate(flops=flops, bytes_accessed=N * B * (F * 4 + D * 12), transcendentals=0),
        name='pipe',
    )(x, g, w1, w2)


def _grad_kernel(S, V, M, B, D, F, FB, KM,
                 x, g, hs, dys, us, dzs, yo, dxo,
                 d1, d2, y, dx,
                 abuf, bbuf, acc, stage, asem, bsem, osem, ssem):
    p = lax.axis_index('stage')
    own_h = p == 0
    own_g = p == S - 1
    NF = F // FB
    NB = V * 2 * NF
    NK = M // KM

    def block(i):
        v = lax.div(i, 2 * NF)
        rem = lax.rem(i, 2 * NF)
        return v, lax.div(rem, NF), lax.rem(rem, NF)

    def fcols(f):
        return pl.ds(pl.multiple_of(f * FB, FB), FB)

    def load(i, k, start):
        v, w, f = block(i)
        sl = k % 2
        ms = pl.ds(k * KM, KM)

        def go(src, dst, sem):
            c = pltpu.make_async_copy(src, dst, sem)
            c.start() if start else c.wait()

        if not start:
            go(hs.at[0, ms], abuf.at[sl], asem.at[sl])
            go(hs.at[0, ms], bbuf.at[sl], bsem.at[sl])
            return

        @pl.when((w == 0) & own_h & (v == 0))
        def _():
            go(x.at[ms], abuf.at[sl], asem.at[sl])

        @pl.when((w == 0) & jnp.logical_not(own_h & (v == 0)))
        def _():
            go(hs.at[v, ms], abuf.at[sl], asem.at[sl])

        @pl.when(w == 0)
        def _():
            go(dzs.at[v, ms, :, fcols(f)], bbuf.at[sl], bsem.at[sl])

        @pl.when(w == 1)
        def _():
            go(us.at[v, ms, :, fcols(f)], abuf.at[sl], asem.at[sl])

        @pl.when((w == 1) & own_g & (v == V - 1))
        def _():
            go(g.at[ms], bbuf.at[sl], bsem.at[sl])

        @pl.when((w == 1) & jnp.logical_not(own_g & (v == V - 1)))
        def _():
            go(dys.at[v, ms], bbuf.at[sl], bsem.at[sl])

    def store(i, start):
        v, w, f = block(i)
        sl = lax.rem(i, 2)

        def go(dst):
            c = pltpu.make_async_copy(acc.at[sl], dst, osem.at[sl])
            c.start() if start else c.wait()

        if not start:
            go(d1.at[0, :, pl.ds(0, FB)])
            return

        @pl.when(w == 0)
        def _():
            go(d1.at[v, :, fcols(f)])

        @pl.when(w == 1)
        def _():
            go(d2.at[v, fcols(f), :])

    def pass_copies(m, out):
        if out:
            return (pltpu.make_async_copy(stage.at[0], y.at[m], ssem.at[0]),
                    pltpu.make_async_copy(stage.at[1], dx.at[m], ssem.at[1]))
        return (pltpu.make_async_copy(yo.at[m], stage.at[0], ssem.at[0]),
                pltpu.make_async_copy(dxo.at[m], stage.at[1], ssem.at[1]))

    load(0, 0, True)

    def step(i, carry):
        sl = lax.rem(i, 2)
        has_pass = i < M

        @pl.when(has_pass)
        def _():
            for c in pass_copies(lax.rem(i, M), False):
                c.start()

        @pl.when(i >= 2)
        def _():
            store(i - 2, False)

        for k in range(NK):
            if k + 1 < NK:
                load(i, k + 1, True)
            else:
                @pl.when(i + 1 < NB)
                def _():
                    load(i + 1, 0, True)
            load(i, k, False)
            part = lax.dot_general(abuf[k % 2].reshape(KM * B, D), bbuf[k % 2].reshape(KM * B, FB), TN,
                                   preferred_element_type=F32)
            if k == 0:
                acc[sl] = part
            else:
                acc[sl] += part
            if k == 0:
                @pl.when(has_pass)
                def _():
                    for c in pass_copies(lax.rem(i, M), False):
                        c.wait()
                    for c in pass_copies(lax.rem(i, M), True):
                        c.start()

        @pl.when(has_pass)
        def _():
            for c in pass_copies(lax.rem(i, M), True):
                c.wait()

        store(i, True)
        return carry

    lax.fori_loop(0, NB, step, 0)
    store(NB - 2, False)
    store(NB - 1, False)


def _grads(x, g, hs, dys, us, dzs, yo, dxo, S):
    V, M, B, F = us.shape
    D = x.shape[2]
    FB = D
    KM = M // 2
    NB = V * 2 * (F // FB)
    assert NB >= M and (M // KM) % 2 == 0
    kern = functools.partial(_grad_kernel, S, V, M, B, D, F, FB, KM)
    DMA = pltpu.SemaphoreType.DMA
    return pl.pallas_call(
        kern,
        out_shape=(jax.ShapeDtypeStruct((V, D, F), F32), jax.ShapeDtypeStruct((V, F, D), F32),
                   jax.ShapeDtypeStruct((M, B, D), BF), jax.ShapeDtypeStruct((M, B, D), BF)),
        in_specs=[pl.BlockSpec(memory_space=ANY)] * 8,
        out_specs=[pl.BlockSpec(memory_space=ANY)] * 4,
        scratch_shapes=[
            pltpu.VMEM((2, KM, B, D), BF), pltpu.VMEM((2, KM, B, FB), BF), pltpu.VMEM((2, D, FB), F32),
            pltpu.VMEM((2, B, D), BF), DMA((2,)), DMA((2,)), DMA((2,)), DMA((2,)),
        ],
        compiler_params=pltpu.CompilerParams(vmem_limit_bytes=VMEM_LIMIT),
        cost_estimate=pl.CostEstimate(flops=V * M * 4 * B * D * F, bytes_accessed=V * M * B * (4 * F + 4 * D),
                                      transcendentals=0),
        name='grads',
    )(x, g, hs, dys, us, dzs, yo, dxo)


def solution(mesh):
    S = mesh.shape['stage']

    def body(x, g, w1, w2):
        w1 = w1[:, 0]
        w2 = w2[:, 0]
        hs, dys, us, dzs, yo, dxo = _pipe(x, g, w1, w2, S)
        d1, d2, y, dx = _grads(x, g, hs, dys, us, dzs, yo, dxo, S)
        return y, dx, d1[:, None], d2[:, None]

    act = P('data', None, None)
    wsp = P(None, 'stage', None, None)
    gsp = P('data', 'stage', None, None)
    return jax.shard_map(body, mesh=mesh, in_specs=(act, act, wsp, wsp), out_specs=(act, act, gsp, gsp), check_vma=False)
```

time: 3990 us -> 1230 us (0.31)
  matrix products: 2320 us -> 0 us
  Pallas kernels: 0 us -> 1220 us
  waiting for transfers between devices: 818 us -> 0 us
  other arithmetic: 387 us -> 0 us
  local copies, waits for them, and re-layouts: 386 us -> 0 us
  starting transfers between devices: 47.4 us -> 0 us
    dot_general x160 -> x0, matrix products: 2320 us -> none  [the longest x35 593 us: _fwd(): r = jnp.dot(u, w2, preferred_element_type=jnp.float32)]
    pallas_call x0 -> x2, Pallas kernels: none -> 1220 us  [the longest x1 929 us: _pipe(): pl.pallas_call(kern, out_shape=(act, act, wide, wide, out, out), in_specs...]
    psum x1 -> x0, waiting for transfers between devices: 473 us -> none  [body(): y = lax.psum(ybuf, 'stage')]
    ppermute x68 -> x0, waiting for transfers between devices: 345 us -> none  [the longest x34 318 us: body(): recv = lax.ppermute(hout, 'stage', fwd_pairs)]
    another operation x58 -> x0, other arithmetic: 179 us -> none  [the longest x18 148 us: _acc(): h, u, dz, dy = [jnp.stack([r[k] for r in rows]) for k in range(2, 6)]]
    scatter x35 -> x0, other arithmetic: 143 us -> none  [body(): saved = saved.at[v, m].set(jnp.where(valid, hin, saved[v, m]))]
    dynamic_slice x102 -> x0, local copies, waits for them, and re-layouts: 141 us -> none  [the longest x34 51.9 us: body(): dxbuf = dxbuf.at[m].set(jnp.where(valid & first & (v == 0), dh, dxbuf[m]))]
    another operation x30 -> x0, local copies, waits for them, and re-layouts: 90.2 us -> none  [the longest x28 77.4 us: _acc(): h, u, dz, dy = [jnp.stack([r[k] for r in rows]) for k in range(2, 6)]]
  transfers between devices with their start and end apart: 69 -> 0, of which waited for: 39 -> 0; matrix products, arithmetic and copies ran while one was open for 31% -> 0% of each run, Pallas kernels for 0% -> 0%
where the time goes in v1:
time: 1230 us; the launch traced here: 1220 us
  Pallas kernels  1220 us (99%)
    pallas_call x1, Pallas kernels, _pipe(): pl.pallas_call(kern, out_shape=(act, act, wide, wide, out, out), in_specs...  929 us
    pallas_call x1, Pallas kernels, _grads(): pl.pallas_call(kern, out_shape=(jax.ShapeDtypeStruct((V, D, F), F32), jax...  291 us

profile of v1, /device:TPU:0, one launch (start us, length us, event | category | flops | bytes accessed | tf_op | source)
XLA Modules:
  0.0 1221.4 jit_solution(7015543949778853639)
XLA Ops:
  0.6 929.1 %pipe.1 = (bf16[2,16,512,1024]{3,2,1,0:T(8,128)(2,1)}, bf16[2,16,512,1024]{3,2,1,0:T(8,128)(2,1)}, bf16[2,16,512,4096]{3,2,1,0:T(8,128)(2,1)}, bf16[2,16,512,409...) custom-call(bf16[16,512,1024]{2,1,0:T(8,128)(2,1)} %x.3, ...), custom_call_target="tpu_custom_call" | custom-call | flops 687194767360 | bytes 469762048 | tf_op jit(solution)/shard_map/pipe/pallas_call | solution.py:384
  929.8 291.5 %grads.1 = (f32[2,1024,4096]{2,1,0:T(8,128)}, f32[2,4096,1024]{2,1,0:T(8,128)}, bf16[16,512,1024]{2,1,0:T(8,128)(2,1)}, bf16[16,512,1024]{2,1,0:T(8,128)(2,1)}) custom-call(bf16[16,512,1024]{2,1,0:T(8,128)(2,1)} %x.3, bf16[16,512,1024]{2,1,0:T(8,128)(2,1)} %g.3, bf16[2,16,512,1024]{3,2,1,0:T(8,128)(2,1)} %get-tuple-element.14.hs, ...), custom_call_target="tpu_custom_call" | custom-call | flops 274877906944 | bytes 335544320 | tf_op jit(solution)/shard_map/grads/pallas_call | solution.py:546
